TPU v7x, 32 devices: a whole 2x2x4 slice. The times are simulated.
32 devices in a mesh: seq: 8 (over z, core), fsdp: 4 (over y, x).
Axes of the slice: x: 2, y: 2, z: 4, core: 2. Of those that a mesh axis runs over, the one named last changes fastest.
Arguments:
- patches: bfloat16 [4, 1024, 3072], P('fsdp', 'seq'), may hold values from -6 to 6
- weight_codes: int32 [3072, 3072], P('fsdp'), may hold values from -448 to 448
- block_scales: float32 [24, 24], P('fsdp'), may hold values from 2.5e-05 to 0.0001
- key_proj: bfloat16 [4, 1024, 3072], P('fsdp', 'seq'), may hold values from -6 to 6
- value_proj: bfloat16 [4, 1024, 3072], P('fsdp', 'seq'), may hold values from -6 to 6
- query_gain: float32 [3072], replicated, may hold values from 1 to 10
- key_gain: float32 [3072], replicated, may hold values from 1 to 10
Outputs:
- attended: bfloat16 [4, 1024, 3072], P('fsdp', 'seq')
All inputs are finite; a program needn't handle non-finite values.
Results may differ from a plain program's by a relative error of at most 0.007.
The roundings to bfloat16 on the way count: a program that leaves them out, or rounds other values in their place, can miss the bound.
Values may be sent and summed in bfloat16 or wider, within the bound.
A program may use at most 192 MiB of HBM per device.

v0:
```python
import jax
import jax.numpy as jnp
from jax import lax
from jax.sharding import PartitionSpec as P

HEADS = 48
HDIM = 64
BLOCK = 128


NORM_FLOOR = 0.25


def head_norm(projected, gain_row):
    shaped = projected.reshape(projected.shape[:-1] + (HEADS, HDIM))
    average = jnp.mean(shaped, axis=-1, keepdims=True)
    centred = shaped - average
    spread = jnp.mean(centred * centred, axis=-1, keepdims=True)
    normed = centred * lax.rsqrt(spread + NORM_FLOOR) * gain_row.reshape(HEADS, HDIM)
    return normed.astype(jnp.bfloat16)


def dequantize(weight_codes, block_scales):
    row_count, column_count = weight_codes.shape
    blocked = weight_codes.astype(jnp.float32).reshape(
        row_count // BLOCK, BLOCK, column_count // BLOCK, BLOCK
    )
    return (
        (blocked * block_scales[:, None, :, None])
        .reshape(row_count, column_count)
        .astype(jnp.bfloat16)
    )


def start_of(query_view):
    image_count, token_count, head_count = (
        query_view.shape[0],
        query_view.shape[1],
        query_view.shape[2],
    )
    return (
        jnp.full((image_count, token_count, head_count), -1e30, jnp.float32),
        jnp.zeros((image_count, token_count, head_count), jnp.float32),
        jnp.zeros(query_view.shape, jnp.float32),
    )


def attend_block(query_view, state_now, key_view, value_view):
    running_max, running_sum, weighted = state_now
    scores = jnp.einsum(
        "ithd,ishd->iths", query_view, key_view, preferred_element_type=jnp.float32
    ) * HDIM ** (-0.5)
    newest = jnp.maximum(running_max, jnp.max(scores, axis=-1))
    probability = jnp.exp(scores - newest[..., None])
    running_sum = jnp.sum(probability, axis=-1)
    blended = jnp.einsum(
        "iths,ishd->ithd",
        probability.astype(jnp.bfloat16),
        value_view,
        preferred_element_type=jnp.float32,
    )
    weighted = blended
    return (newest, running_sum, weighted)


def per_device(patches, weight_codes, block_scales, key_proj, value_proj, query_gain, key_gain):
    image_count, token_count, feature_count = patches.shape
    flat_rows = patches.reshape(image_count * token_count, feature_count)
    key_norm = head_norm(key_proj.astype(jnp.float32), key_gain)
    value_view = value_proj.reshape(image_count, token_count, HEADS, HDIM)
    local_weight = dequantize(weight_codes, block_scales)
    group_rows = lax.all_to_all(flat_rows, "fsdp", split_axis=1, concat_axis=0, tiled=True)
    queries = lax.psum_scatter(
        jnp.dot(group_rows, local_weight, preferred_element_type=jnp.float32),
        "fsdp",
        scatter_dimension=0,
        tiled=True,
    )
    query_view = head_norm(queries, query_gain).reshape(image_count, token_count, HEADS, HDIM)
    finished = attend_block(
        query_view,
        start_of(query_view),
        lax.all_gather(key_norm, "seq", axis=1, tiled=True),
        lax.all_gather(value_view, "seq", axis=1, tiled=True),
    )
    attended = finished[2] / finished[1][..., None]
    return attended.reshape(image_count, token_count, HEADS * HDIM).astype(jnp.bfloat16)


def solution(mesh):
    in_specs = (
        P("fsdp", "seq", None),
        P("fsdp", None),
        P("fsdp", None),
        P("fsdp", "seq", None),
        P("fsdp", "seq", None),
        P(),
        P(),
    )
    out_specs = P("fsdp", "seq", None)
    return jax.shard_map(
        per_device, mesh=mesh, in_specs=in_specs, out_specs=out_specs, check_vma=False
    )
```

profile of v0, /device:TPU:0, one launch (start us, length us, event | category | flops | bytes accessed | tf_op | source)
XLA Modules:
  0.0 192.2 jit_solution(13394318561025549353)
XLA Ops:
  7.4 1.5 copy.17
  8.9 16.3 %all_to_all.19 = bf16[128,4,768]{0,2,1:T(8,128)(2,1)S(1)} all-to-all(bf16[128,4,768]{0,2,1:T(8,128)(2,1)S(1)} %bitcast.66), channel_id=1, replica_groups=mesh['seq'=8,'fsdp'=4] {'fsdp'}, dimensions={1} | all-to-all | bytes 1572864 | tf_op jit(solution)/shard_map/all_to_all | solution.py:72
  25.2 0.3 copy.18
  25.5 0.0 copy-start
  25.5 1.5 mul.102
  27.0 2.2 %copy-done = s32[768,3072]{1,0:T(8,128)S(1)} copy-done((s32[768,3072]{1,0:T(8,128)S(1)}, s32[768,3072]{1,0:T(8,128)}, u32[]{:S(2)}) %copy-start) | copy-done | bytes 9437208
  29.2 6.4 %convolution_bitcast_fusion = f32[512,3072]{0,1:T(8,128)} fusion(bf16[512,768]{1,0:T(8,128)(2,1)S(1)} %bitcast.67, f32[96,8,24,128]{3,2,1,0:T(8,128)S(1)} %bitcast.57, s32[768,3072]{1,0:T(8,128)S(1)} %copy-done), kind=kOutput, calls=%fused_computation.14 | convolution fusion | flops 2422996992 | bytes 25952256 | tf_op jit(solution)/shard_map/dot_general | solution.py:74
  35.6 0.0 reduce-scatter.2.cloned.1.call-update
  35.6 0.0 copy-start.2
  35.7 0.0 copy-start.4
  35.7 0.0 all-gather.3.cloned.1.call-start
  35.7 1.0 copy-done.1
  36.7 0.4 copy.16
  37.1 0.1 convert_element_type.42
  37.3 0.1 mul.99
  37.3 0.2 reduce_sum.45
  37.5 0.3 multiply_reduce_fusion.1
  37.9 1.4 multiply_convert_fusion.1
  39.2 0.0 all-gather.3.cloned.1.call-update
  39.3 0.2 all-gather.5.cloned.1.call-start
  39.5 1.1 copy.19
  40.7 0.0 all-gather.5.cloned.1.call-update
  40.7 0.1 mul.108
  40.8 64.8 %reduce-scatter.2.cloned.1.call-done = f32[128,3072]{0,1:T(8,128)} async-done(((f32[512,3072]{0,1:T(8,128)}), f32[128,3072]{0,1:T(8,128)}) %reduce-scatter.2.cloned.1.call-update) | async-done | bytes 1572880 | tf_op jit(solution)/shard_map/reduce_scatter | solution.py:73
  105.6 1.6 reduce_sum.47
  107.2 1.7 multiply_reduce_fusion
  108.9 0.0 all-gather.3.cloned.1.call-done
  108.9 13.5 %bitcast_reduce_fusion = (f32[128,48]{0,1:T(8,128)S(1)}, f32[48,1024,128]{2,1,0:T(8,128)}) fusion(f32[128,48,64]{0,2,1:T(8,128)} %bitcast.63, f32[48,64]{1,0:T(8,128)S(1)} %mul.108, f32[128,48]{0,1:T(8,128)S(1)} %add_rsqrt_fusion, f32[128,48]{0,1:T(8,128)S(1)} %broadcast_multiply_fusion, bf16[1,1024,48,64]{1,3,2,0:T(8,128)(2,1)} %all-gather.3.cloned.1.call-done), kind=kOutput, calls=%fused_computation.1 | convolution fusion | flops 819456000 | bytes 33116160 | tf_op jit(solution)/shard_map/ithd,ishd->iths/dot_general | solution.py:50
  122.5 10.6 %fusion.1 = f32[128,48]{0,1:T(8,128)S(1)} fusion(f32[48,1024,128]{2,1,0:T(8,128)} %get-tuple-element.6, f32[128,48]{0,1:T(8,128)S(1)} %broadcast_maximum_fusion), kind=kLoop, calls=%fused_computation.3 | loop fusion | flops 18868224 | bytes 25214976 | tf_op jit(solution)/shard_map/reduce_sum | solution.py:55
  133.1 35.7 %all-gather.5.cloned.1.call-done = bf16[1,1024,48,64]{1,3,2,0:T(8,128)(2,1)} async-done(((bf16[1,128,48,64]{1,3,2,0:T(8,128)(2,1)}), bf16[1,1024,48,64]{1,3,2,0:T(8,128)(2,1)}) %all-gather.5.cloned.1.call-update) | async-done | bytes 6291472 | tf_op jit(solution)/shard_map/all_gather | solution.py:84
  168.8 14.8 %fusion.13 = bf16[1,128,48,64]{1,3,2,0:T(8,128)(2,1)S(1)} fusion(f32[48,1024,128]{2,1,0:T(8,128)} %get-tuple-element.6, f32[128,48]{0,1:T(8,128)S(1)} %broadcast_maximum_fusion, bf16[1,1024,48,64]{1,3,2,0:T(8,128)(2,1)} %all-gather.5.cloned.1.call-done, f32[128,48]{0,1:T(8,128)S(1)} %fusion.1), kind=kOutput, calls=%fused_computation.16 | convolution fusion | flops 824967168 | bytes 32292864 | tf_op jit(solution)/shard_map/iths,ishd->ithd/dot_general | solution.py:56
  183.6 1.2 copy.21
  (11 shorter events, 0.0 us)
Async XLA Ops:
  7.4 98.2 %reduce-scatter.2.cloned.1.call-start = ((), (), s32[]{:S(2)}) async-start(), calls=%async_computation.3 | async-start | bytes 7864320 | tf_op jit(solution)/shard_map/reduce_scatter | solution.py:73
  25.5 3.7 %copy-start = (s32[768,3072]{1,0:T(8,128)S(1)}, s32[768,3072]{1,0:T(8,128)}, u32[]{:S(2)}) copy-start(s32[768,3072]{1,0:T(8,128)} %param.8) | copy-start | bytes 28311556
  35.6 1.1 copy-start.1
  35.6 1.6 copy-start.3
  35.6 3.9 %copy-start.2 = (bf16[1,128,3072]{2,1,0:T(8,128)(2,1)S(1)}, bf16[1,128,3072]{2,1,0:T(8,128)(2,1)}, u32[]{:S(2)}) copy-start(bf16[1,128,3072]{2,1,0:T(8,128)(2,1)} %param.11) | copy-start | bytes 2359300
  35.7 5.0 %copy-start.4 = (f32[3072]{0:T(1024)S(1)}, f32[3072]{0:T(1024)}, u32[]{:S(2)}) copy-start(f32[3072]{0:T(1024)} %param.12) | copy-start | bytes 36868
  35.7 73.3 %all-gather.3.cloned.1.call-start = ((), (), s32[]{:S(2)}) async-start(), calls=%async_computation.2 | async-start | bytes 7077888 | tf_op jit(solution)/shard_map/all_gather | solution.py:83
  39.3 129.6 %all-gather.5.cloned.1.call-start = ((), (), s32[]{:S(2)}) async-start(), calls=%async_computation.4 | async-start | bytes 7077888 | tf_op jit(solution)/shard_map/all_gather | solution.py:84
Sparse Core Ops, SparseCore 0:
  35.8 69.7 reduce-scatter.1
Sparse Core Ops, SparseCore 1:
  39.4 64.7 all-gather.2
  105.6 63.2 all-gather.4
where the time goes:
time: 193 us; the launch traced here: 192 us
  waiting for transfers between devices  101 us (52%)
  matrix products  34.7 us (18%)
  blocking collectives  16.3 us (8%)
  other arithmetic  16 us (8%)
  between operations  15 us (8%)
  local copies, waits for them, and re-layouts  9.35 us (5%)
    reduce_scatter x1, waiting for transfers between devices, per_device(): lax.psum_scatter(jnp.dot(group_rows, local_weight, preferred_element_type...  64.8 us
    all_gather x1, waiting for transfers between devices, per_device(): lax.all_gather(value_view, 'seq', axis=1, tiled=True)  35.7 us
    all_to_all x1, blocking collectives, per_device(): lax.all_to_all(flat_rows, 'fsdp', split_axis=1, concat_axis=0, tiled=True)  16.3 us
    dot_general x1, matrix products, attend_block(): jnp.einsum('iths,ishd->ithd', probability.astype(jnp.bfloat16), value_vie...  14.8 us
    dot_general x1, matrix products, attend_block(): jnp.einsum('ithd,ishd->iths', query_view, key_view, preferred_element_typ...  13.5 us
    reduce_sum x1, other arithmetic, attend_block(): running_sum = jnp.sum(probability, axis=-1)  10.6 us
    dot_general x1, matrix products, per_device(): jnp.dot(group_rows, local_weight, preferred_element_type=jnp.float32)  6.42 us
    unnamed x13, local copies, waits for them, and re-layouts  6.24 us
  transfers between devices with their start and end apart: 3, of which 2 were waited for; matrix products, arithmetic and copies ran while one was open for 16% of the time, Pallas kernels for 0%

commit v1 on v0

--- a/solution.py
+++ b/solution.py
@@ -1,6 +1,10 @@
+import functools
+import math
 import jax
 import jax.numpy as jnp
 from jax import lax
+from jax.experimental import pallas as pl
+from jax.experimental.pallas import tpu as pltpu
 from jax.sharding import PartitionSpec as P
 
 HEADS = 48
@@ -87,17 +91,270 @@
     return attended.reshape(image_count, token_count, HEADS * HDIM).astype(jnp.bfloat16)
 
 
+MESH = pl.DeviceIdType.MESH
+LANES = 128
+CORES = 2
+
+
+def column_norm(values, gain_row):
+    lane = lambda axis: lax.broadcasted_iota(jnp.int32, (LANES, LANES), axis) < HDIM
+    spread_out = jnp.where(lane(0) == lane(1), 1.0 / HDIM, 0.0).astype(jnp.float32)
+    mean_of = lambda t: jnp.dot(t, spread_out, preferred_element_type=jnp.float32, precision=lax.Precision.HIGHEST)
+    centred = values - mean_of(values)
+    normed = centred * lax.rsqrt(mean_of(centred * centred) + NORM_FLOOR) * gain_row
+    return normed.astype(jnp.bfloat16)
+
+
+def fused_kernel(
+    n, fn, patches, codes, scales, key, value, query_gain, key_gain, out,
+    pbuf, cbuf, wbuf, kraw, vbuf, knorm, qsend, qbuf, obuf,
+    local_sem, code_sem, p_send, p_recv, fw_send, fw_recv, w_send, w_recv,
+    kv_send, kv_recv, q_send, q_recv, o_send, o_recv, own_sem,
+):
+    s, f = lax.axis_index("seq"), lax.axis_index("fsdp")
+    m = n // 2
+    half, place = s // m, lax.rem(s, m)
+    tokens = patches.shape[0]
+    rows, columns = codes.shape
+    width = columns // n
+    chunks = width // LANES
+    group = m * tokens
+    chips = m // CORES
+    partner = s + 1 - 2 * lax.rem(s, CORES)
+
+    def chip_mate(d):
+        return half * m + lax.rem(place + d * CORES, m)
+
+    def rows_of(device):
+        return pl.ds(pl.multiple_of(lax.rem(device, m) * tokens, tokens), tokens)
+
+    def all_rows_of(device):
+        return pl.ds(pl.multiple_of(device * tokens, tokens), tokens)
+
+    def owned(device):
+        return pl.multiple_of((lax.rem(device, m) * 2 + device // m) * width, LANES)
+
+    def chunk_column(q):
+        side = jnp.where(q < chunks, 1 - half, half)
+        return pl.multiple_of((place * 2 + side) * width + lax.rem(q, chunks) * LANES, LANES)
+
+    code_copies = []
+    for q in range(2 * chunks):
+        code_copies.append(pltpu.make_async_copy(
+            codes.at[:, pl.ds(chunk_column(q), LANES)], cbuf.at[q], code_sem.at[q]))
+        code_copies[-1].start()
+    own_copies = [
+        pltpu.make_async_copy(patches, pbuf.at[rows_of(s)], local_sem.at[0]),
+        pltpu.make_async_copy(key.at[:, pl.ds(owned(s), width)], kraw.at[all_rows_of(s)], local_sem.at[1]),
+        pltpu.make_async_copy(value.at[:, pl.ds(owned(s), width)], vbuf.at[all_rows_of(s)], local_sem.at[2]),
+    ]
+    for copy in own_copies:
+        copy.start()
+
+    barrier = pltpu.get_barrier_semaphore()
+    for d in range(1, n):
+        pl.semaphore_signal(barrier, inc=1, device_id={"seq": lax.rem(s + d, n)}, device_id_type=MESH)
+    for d in range(1, fn):
+        pl.semaphore_signal(barrier, inc=1, device_id={"fsdp": lax.rem(f + d, fn)}, device_id_type=MESH)
+    pl.semaphore_wait(barrier, n - 1 + fn - 1)
+
+    def remote(src, dst, send, recv, **device):
+        return pltpu.make_async_remote_copy(
+            src_ref=src, dst_ref=dst, send_sem=send, recv_sem=recv, device_id=device, device_id_type=MESH)
+
+    patch_copies = [remote(patches, pbuf.at[rows_of(s)], p_send.at[0], p_recv.at[0], seq=partner)]
+    for d in range(1, chips):
+        patch_copies.append(remote(patches, pbuf.at[rows_of(s)], p_send.at[d], p_recv.at[d], seq=chip_mate(d)))
+    for copy in patch_copies[1:] + patch_copies[:1]:
+        copy.start()
+    kv_copies = []
+    for which, (src, dst) in enumerate(((key, kraw), (value, vbuf))):
+        for d in range(1, n):
+            to = lax.rem(s + d, n)
+            kv_copies.append(remote(
+                src.at[:, pl.ds(owned(to), width)], dst.at[all_rows_of(s)],
+                kv_send.at[which, d], kv_recv.at[which, d], seq=to))
+            kv_copies[-1].start()
+
+    own_rows = pl.ds(pl.multiple_of(f * rows, rows), rows)
+
+    def weight_copies(q):
+        return [
+            remote(wbuf.at[q, own_rows], wbuf.at[q, own_rows], w_send.at[q, d], w_recv.at[q, d],
+                   fsdp=lax.rem(f + d, fn))
+            for d in range(1, fn)
+        ]
+
+    def dequantize_chunk(q, _):
+        pltpu.make_async_copy(
+            codes.at[:, pl.ds(chunk_column(q), LANES)], cbuf.at[q], code_sem.at[q]).wait()
+        for block in range(rows // BLOCK):
+            scale = scales[block, chunk_column(q) // BLOCK]
+            piece = cbuf[q, block * BLOCK:(block + 1) * BLOCK, :].astype(jnp.float32) * scale
+            wbuf[q, pl.ds(pl.multiple_of(f * rows + block * BLOCK, BLOCK), BLOCK), :] = piece.astype(jnp.bfloat16)
+        for copy in weight_copies(q):
+            copy.start()
+        return 0
+
+    lax.fori_loop(0, 2 * chunks, dequantize_chunk, 0)
+
+    own_copies[0].wait()
+    forwards = []
+    for d in range(1, chips):
+        patch_copies[d].wait()
+        came_from = half * m + lax.rem(place + m - d * CORES, m)
+        forwards.append(remote(
+            pbuf.at[rows_of(came_from)], pbuf.at[rows_of(came_from)], fw_send.at[d], fw_recv.at[d], seq=partner))
+        forwards[-1].start()
+    patch_copies[0].wait()
+    for copy in forwards:
+        copy.wait()
+
+    def project(q):
+        for copy in weight_copies(q):
+            copy.wait()
+        queries = jnp.dot(pbuf[...], wbuf[q], preferred_element_type=jnp.float32)
+        return column_norm(queries, query_gain[:, pl.ds(chunk_column(q), LANES)])
+
+    other = lax.rem(s + m, n)
+    half_rows = pl.ds(pl.multiple_of(half * group, group), group)
+
+    def query_copy(k):
+        return remote(qsend.at[k], qbuf.at[k, half_rows], q_send.at[k], q_recv.at[k], seq=other)
+
+    def exchange_chunk(k, _):
+        qsend[k] = project(k)
+        query_copy(k).start()
+        return 0
+
+    lax.fori_loop(0, chunks, exchange_chunk, 0)
+
+    own_copies[1].wait()
+    own_copies[2].wait()
+    for copy in kv_copies:
+        copy.wait()
+
+    def key_chunk(k, _):
+        at = pl.multiple_of(k * LANES, LANES)
+        knorm[k] = column_norm(
+            kraw[:, pl.ds(at, LANES)].astype(jnp.float32),
+            key_gain[:, pl.ds(pl.multiple_of(owned(s) + at, LANES), LANES)])
+        return 0
+
+    lax.fori_loop(0, chunks, key_chunk, 0)
+
+    tile = 2 * tokens
+    exponent = HDIM ** (-0.5) * math.log2(math.e)
+
+    def out_columns(k):
+        return pl.ds(pl.multiple_of(owned(s) + k * LANES, LANES), LANES)
+
+    def out_copies(k):
+        return [
+            remote(obuf.at[k, all_rows_of(lax.rem(s + d, n))], out.at[:, out_columns(k)],
+                   o_send.at[k, d], o_recv.at[k, d], seq=lax.rem(s + d, n))
+            for d in range(1, n)
+        ]
+
+    def own_out(k):
+        return pltpu.make_async_copy(obuf.at[k, all_rows_of(s)], out.at[:, out_columns(k)], own_sem.at[k])
+
+    def attend_chunk(k, _):
+        qbuf[k, half_rows] = project(chunks + k)
+        query_copy(k).wait()
+        values = vbuf[:, pl.ds(pl.multiple_of(k * LANES, LANES), LANES)]
+        keys = knorm[k]
+        first = lax.broadcasted_iota(jnp.int32, (tile, LANES), 1) < HDIM
+
+        def attend_tile(i, _):
+            here = pl.ds(pl.multiple_of(i * tile, tile), tile)
+            queries = qbuf[k, here]
+            results = []
+            for mine in (first, jnp.logical_not(first)):
+                masked = jnp.where(mine, queries, jnp.zeros_like(queries))
+                scores = lax.dot_general(
+                    masked, keys, (((1,), (1,)), ((), ())), preferred_element_type=jnp.float32)
+                largest = jnp.max(scores, axis=-1, keepdims=True)
+                probability = jnp.exp2((scores - largest) * exponent)
+                normaliser = jnp.sum(probability, axis=-1, keepdims=True)
+                blended = jnp.dot(
+                    probability.astype(jnp.bfloat16), values, preferred_element_type=jnp.float32)
+                results.append(blended / normaliser)
+            obuf[k, here] = jnp.where(first, results[0], results[1]).astype(jnp.bfloat16)
+            return 0
+
+        lax.fori_loop(0, n * tokens // tile, attend_tile, 0)
+        own_out(k).start()
+        for copy in out_copies(k):
+            copy.start()
+        return 0
+
+    lax.fori_loop(0, chunks, attend_chunk, 0)
+
+    def finish(k, _):
+        own_out(k).wait()
+        for copy in out_copies(k):
+            copy.wait()
+        return 0
+
+    lax.fori_loop(0, chunks, finish, 0)
+
+
+def fused_per_device(n, fn, patches, weight_codes, block_scales, key_proj, value_proj, query_gain, key_gain):
+    _, tokens, features = patches.shape
+    rows, columns = weight_codes.shape
+    width = columns // n
+    chunks = width // LANES
+    group = n // 2 * tokens
+    bf16 = jnp.bfloat16
+    dma = pltpu.SemaphoreType.DMA
+    anywhere = pl.BlockSpec(memory_space=pl.ANY)
+    vmem = pl.BlockSpec(memory_space=pltpu.VMEM)
+    result = pl.pallas_call(
+        functools.partial(fused_kernel, n, fn),
+        out_shape=jax.ShapeDtypeStruct((tokens, columns), bf16),
+        in_specs=[anywhere, anywhere, pl.BlockSpec(memory_space=pltpu.SMEM), anywhere, anywhere, vmem, vmem],
+        out_specs=anywhere,
+        scratch_shapes=[
+            pltpu.VMEM((group, features), bf16),
+            pltpu.VMEM((2 * chunks, rows, LANES), jnp.int32),
+            pltpu.VMEM((2 * chunks, features, LANES), bf16),
+            pltpu.VMEM((n * tokens, width), bf16),
+            pltpu.VMEM((n * tokens, width), bf16),
+            pltpu.VMEM((chunks, n * tokens, LANES), bf16),
+            pltpu.VMEM((chunks, group, LANES), bf16),
+            pltpu.VMEM((chunks, n * tokens, LANES), bf16),
+            pltpu.VMEM((chunks, n * tokens, LANES), bf16),
+            dma((3,)), dma((2 * chunks,)),
+            dma((n,)), dma((n,)), dma((n,)), dma((n,)),
+            dma((2 * chunks, fn)), dma((2 * chunks, fn)),
+            dma((2, n)), dma((2, n)),
+            dma((chunks,)), dma((chunks,)),
+            dma((chunks, n)), dma((chunks, n)), dma((chunks,)),
+        ],
+        compiler_params=pltpu.CompilerParams(
+            collective_id=0, has_side_effects=True, vmem_limit_bytes=56 * 1024 * 1024),
+    )(
+        patches.reshape(tokens, features), weight_codes, block_scales,
+        key_proj.reshape(tokens, columns), value_proj.reshape(tokens, columns),
+        query_gain.reshape(1, columns), key_gain.reshape(1, columns),
+    )
+    return result.reshape(1, tokens, columns)
+
+
 def solution(mesh):
-    in_specs = (
-        P("fsdp", "seq", None),
-        P("fsdp", None),
-        P("fsdp", None),
-        P("fsdp", "seq", None),
-        P("fsdp", "seq", None),
-        P(),
-        P(),
-    )
-    out_specs = P("fsdp", "seq", None)
-    return jax.shard_map(
-        per_device, mesh=mesh, in_specs=in_specs, out_specs=out_specs, check_vma=False
-    )
+    n, fn = mesh.shape["seq"], mesh.shape["fsdp"]
+    specs = (
+        P("fsdp", "seq", None), P("fsdp", None), P("fsdp", None),
+        P("fsdp", "seq", None), P("fsdp", "seq", None), P(), P(),
+    )
+
+    def whole(*arrays):
+        patches, weight_codes = arrays[:2]
+        fits = patches.shape[0] == fn and weight_codes.shape[1] % (n * LANES) == 0 and n % (2 * CORES) == 0
+        body = functools.partial(fused_per_device, n, fn) if fits else per_device
+        return jax.shard_map(
+            body, mesh=mesh, in_specs=specs, out_specs=P("fsdp", "seq", None), check_vma=False
+        )(*arrays)
+
+    return whole

time: 193 us -> 88.5 us (0.46)
  waiting for transfers between devices: 101 us -> 0 us
  Pallas kernels: 0 us -> 86.2 us
  matrix products: 34.7 us -> 0 us
  blocking collectives: 16.3 us -> 0 us
  other arithmetic: 16 us -> 0 us
  between operations: 15 us -> 0.01 us
  local copies, waits for them, and re-layouts: 9.35 us -> 2.06 us
    pallas_call x0 -> x1, Pallas kernels: none -> 86.2 us  [fused_per_device(): pl.pallas_call(functools.partial(fused_kernel, n, fn), out_shape=jax.Shap...]
    reduce_scatter x1 -> x0, waiting for transfers between devices: 64.8 us -> none  [per_device(): lax.psum_scatter(jnp.dot(group_rows, local_weight, preferred_element_type...]
    all_gather x2 -> x0, waiting for transfers between devices: 35.7 us -> none  [the longest x1 35.7 us: per_device(): lax.all_gather(value_view, 'seq', axis=1, tiled=True)]
    dot_general x3 -> x0, matrix products: 34.7 us -> none  [the longest x1 14.8 us: attend_block(): jnp.einsum('iths,ishd->ithd', probability.astype(jnp.bfloat16), value_vie...]
    all_to_all x1 -> x0, blocking collectives: 16.3 us -> none  [per_device(): lax.all_to_all(flat_rows, 'fsdp', split_axis=1, concat_axis=0, tiled=True)]
    reduce_sum x5 -> x0, other arithmetic: 14.4 us -> none  [the longest x1 10.6 us: attend_block(): running_sum = jnp.sum(probability, axis=-1)]
    unnamed x13 -> x1, local copies, waits for them, and re-layouts: 6.24 us -> 2.06 us
  transfers between devices with their start and end apart: 3 -> 0, of which waited for: 2 -> 0; matrix products, arithmetic and copies ran while one was open for 16% -> 0% of each run, Pallas kernels for 0% -> 0%
where the time goes in v1:
time: 88.5 us; the launch traced here: 88.2 us
  Pallas kernels  86.2 us (97%)
  local copies, waits for them, and re-layouts  2.06 us (2%)
    pallas_call x1, Pallas kernels, fused_per_device(): pl.pallas_call(functools.partial(fused_kernel, n, fn), out_shape=jax.Shap...  86.2 us
    unnamed x1, local copies, waits for them, and re-layouts  2.06 us

profile of v1, /device:TPU:0, one launch (start us, length us, event | category | flops | bytes accessed | tf_op | source)
XLA Modules:
  0.0 88.2 jit_solution(9730658830762077074)
XLA Ops:
  0.0 86.2 %shard_map.73 = bf16[128,3072]{1,0:T(8,128)(2,1)} custom-call(bf16[128,3072]{1,0:T(8,128)(2,1)} %bitcast.7, s32[768,3072]{1,0:T(8,128)} %codes.1, f32[6,24]{1,0:T(8,128)} %scales.1, bf16[128,3072]{1,0:T(8,128)(2,1)} %bitcast.8, bf16[128,3072]{1,0:T(8,128)(2,1)} %bitcast.9, f32[1,3072]{1,0:T(1,128)} %bitcast.10, f32[1,3072]{1,0:T(1,128)} %bitcast.11), custom_call_target="tpu_custom_call" | custom-call | tf_op jit(solution)/shard_map/pallas_call | solution.py:313
  86.2 2.1 %copy.9 = bf16[1,128,3072]{2,1,0:T(8,128)(2,1)} copy(bf16[1,128,3072]{2,1,0:T(8,128)(2,1)} %bitcast.6) | data formatting | bytes 1572864

commit v2 on v1

--- a/solution.py
+++ b/solution.py
@@ -98,8 +98,14 @@
 
 def column_norm(values, gain_row):
     lane = lambda axis: lax.broadcasted_iota(jnp.int32, (LANES, LANES), axis) < HDIM
-    spread_out = jnp.where(lane(0) == lane(1), 1.0 / HDIM, 0.0).astype(jnp.float32)
-    mean_of = lambda t: jnp.dot(t, spread_out, preferred_element_type=jnp.float32, precision=lax.Precision.HIGHEST)
+    spread_out = jnp.where(lane(0) == lane(1), 1.0 / HDIM, 0.0).astype(jnp.bfloat16)
+    spread_out = jnp.concatenate([spread_out, spread_out], axis=0)
+
+    def mean_of(t):
+        high = t.astype(jnp.bfloat16)
+        low = (t - high.astype(jnp.float32)).astype(jnp.bfloat16)
+        return jnp.dot(jnp.concatenate([high, low], axis=1), spread_out, preferred_element_type=jnp.float32)
+
     centred = values - mean_of(values)
     normed = centred * lax.rsqrt(mean_of(centred * centred) + NORM_FLOOR) * gain_row
     return normed.astype(jnp.bfloat16)
@@ -167,14 +173,28 @@
         patch_copies.append(remote(patches, pbuf.at[rows_of(s)], p_send.at[d], p_recv.at[d], seq=chip_mate(d)))
     for copy in patch_copies[1:] + patch_copies[:1]:
         copy.start()
-    kv_copies = []
-    for which, (src, dst) in enumerate(((key, kraw), (value, vbuf))):
-        for d in range(1, n):
-            to = lax.rem(s + d, n)
-            kv_copies.append(remote(
-                src.at[:, pl.ds(owned(to), width)], dst.at[all_rows_of(s)],
-                kv_send.at[which, d], kv_recv.at[which, d], seq=to))
-            kv_copies[-1].start()
+
+    far = place // CORES == jnp.where(half == 0, 0, chips - 1)
+
+    def kv_copy(which, d):
+        src, dst = ((key, kraw), (value, vbuf))[which]
+        to = lax.rem(s + d, n)
+        return remote(
+            src.at[:, pl.ds(owned(to), width)], dst.at[all_rows_of(s)],
+            kv_send.at[which, d], kv_recv.at[which, d], seq=to)
+
+    def start_kv(behind_patches):
+        for which in range(2):
+            for step in range(1, n):
+                d = jnp.where(half == 0, step, n - step)
+                to = lax.rem(s + d, n)
+                over_pair = jnp.where(to // m == half, to // CORES != s // CORES, far)
+
+                @pl.when(over_pair == behind_patches)
+                def _():
+                    kv_copy(which, d).start()
+
+    start_kv(False)
 
     own_rows = pl.ds(pl.multiple_of(f * rows, rows), rows)
 
@@ -185,36 +205,50 @@
             for d in range(1, fn)
         ]
 
-    def dequantize_chunk(q, _):
-        pltpu.make_async_copy(
-            codes.at[:, pl.ds(chunk_column(q), LANES)], cbuf.at[q], code_sem.at[q]).wait()
-        for block in range(rows // BLOCK):
-            scale = scales[block, chunk_column(q) // BLOCK]
-            piece = cbuf[q, block * BLOCK:(block + 1) * BLOCK, :].astype(jnp.float32) * scale
-            wbuf[q, pl.ds(pl.multiple_of(f * rows + block * BLOCK, BLOCK), BLOCK), :] = piece.astype(jnp.bfloat16)
-        for copy in weight_copies(q):
+    def dequantize_pair(pair, _):
+        for side in range(2):
+            q = 2 * pair + side
+            pltpu.make_async_copy(
+                codes.at[:, pl.ds(chunk_column(q), LANES)], cbuf.at[q], code_sem.at[q]).wait()
+            for block in range(rows // BLOCK):
+                scale = scales[block, chunk_column(q) // BLOCK]
+                piece = cbuf[q, block * BLOCK:(block + 1) * BLOCK, :].astype(jnp.float32) * scale
+                at = pl.ds(pl.multiple_of(f * rows + block * BLOCK, BLOCK), BLOCK)
+                wbuf[pair, at, side * LANES:(side + 1) * LANES] = piece.astype(jnp.bfloat16)
+        for copy in weight_copies(pair):
             copy.start()
         return 0
 
-    lax.fori_loop(0, 2 * chunks, dequantize_chunk, 0)
+    lax.fori_loop(0, chunks, dequantize_pair, 0)
 
     own_copies[0].wait()
-    forwards = []
+
+    def forward_copy(d):
+        at = rows_of(half * m + lax.rem(place + m - d * CORES, m))
+        return remote(pbuf.at[at], pbuf.at[at], fw_send.at[d], fw_recv.at[d], seq=partner)
+
+    def patches_out():
+        for copy in patch_copies[1:]:
+            copy.wait_send()
+        start_kv(True)
+
+    def patches_in():
+        for d in range(1, chips):
+            patch_copies[d].wait_recv()
+            forward_copy(d).start()
+
+    @pl.when(far)
+    def _():
+        patches_out()
+        patches_in()
+
+    @pl.when(jnp.logical_not(far))
+    def _():
+        patches_in()
+
+    patch_copies[0].wait()
     for d in range(1, chips):
-        patch_copies[d].wait()
-        came_from = half * m + lax.rem(place + m - d * CORES, m)
-        forwards.append(remote(
-            pbuf.at[rows_of(came_from)], pbuf.at[rows_of(came_from)], fw_send.at[d], fw_recv.at[d], seq=partner))
-        forwards[-1].start()
-    patch_copies[0].wait()
-    for copy in forwards:
-        copy.wait()
-
-    def project(q):
-        for copy in weight_copies(q):
-            copy.wait()
-        queries = jnp.dot(pbuf[...], wbuf[q], preferred_element_type=jnp.float32)
-        return column_norm(queries, query_gain[:, pl.ds(chunk_column(q), LANES)])
+        forward_copy(d).wait()
 
     other = lax.rem(s + m, n)
     half_rows = pl.ds(pl.multiple_of(half * group, group), group)
@@ -222,17 +256,29 @@
     def query_copy(k):
         return remote(qsend.at[k], qbuf.at[k, half_rows], q_send.at[k], q_recv.at[k], seq=other)
 
-    def exchange_chunk(k, _):
-        qsend[k] = project(k)
-        query_copy(k).start()
-        return 0
-
-    lax.fori_loop(0, chunks, exchange_chunk, 0)
+    def project(pair):
+        for copy in weight_copies(pair):
+            copy.wait()
+        both = jnp.dot(pbuf[...], wbuf[pair], preferred_element_type=jnp.float32)
+        for side in range(2):
+            q = 2 * pair + side
+            normed = column_norm(
+                both[:, side * LANES:(side + 1) * LANES], query_gain[:, pl.ds(chunk_column(q), LANES)])
+            if q < chunks:
+                qsend[q] = normed
+                query_copy(q).start()
+            else:
+                qbuf[q - chunks, half_rows] = normed
+
+    early = (chunks + 2) // 2
+    for pair in range(early):
+        project(pair)
+        if pair == 0:
+            pl.when(jnp.logical_not(far))(patches_out)
 
     own_copies[1].wait()
-    own_copies[2].wait()
-    for copy in kv_copies:
-        copy.wait()
+    for d in range(1, n):
+        kv_copy(0, d).wait()
 
     def key_chunk(k, _):
         at = pl.multiple_of(k * LANES, LANES)
@@ -243,58 +289,75 @@
 
     lax.fori_loop(0, chunks, key_chunk, 0)
 
+    own_copies[2].wait()
+    for d in range(1, n):
+        kv_copy(1, d).wait()
+
     tile = 2 * tokens
     exponent = HDIM ** (-0.5) * math.log2(math.e)
 
     def out_columns(k):
         return pl.ds(pl.multiple_of(owned(s) + k * LANES, LANES), LANES)
 
-    def out_copies(k):
-        return [
-            remote(obuf.at[k, all_rows_of(lax.rem(s + d, n))], out.at[:, out_columns(k)],
-                   o_send.at[k, d], o_recv.at[k, d], seq=lax.rem(s + d, n))
-            for d in range(1, n)
-        ]
+    def out_copy(k, to):
+        d = lax.rem(to - s + n, n)
+        return remote(obuf.at[k, all_rows_of(to)], out.at[:, out_columns(k)],
+                      o_send.at[k, d], o_recv.at[k, d], seq=to)
 
     def own_out(k):
         return pltpu.make_async_copy(obuf.at[k, all_rows_of(s)], out.at[:, out_columns(k)], own_sem.at[k])
 
-    def attend_chunk(k, _):
-        qbuf[k, half_rows] = project(chunks + k)
-        query_copy(k).wait()
+    first = lax.broadcasted_iota(jnp.int32, (tile, LANES), 1) < HDIM
+    tiles = n // CORES
+
+    def attend_step(step, _):
+        k, i = step // tiles, lax.rem(step, tiles)
+        own_side = half * chips + lax.rem(place // CORES + 1 + i, chips)
+        chip = jnp.where(i < chips, (1 - half) * chips + i, own_side)
+        here = pl.ds(pl.multiple_of(chip * tile, tile), tile)
+
+        @pl.when(i == 0)
+        def _():
+            query_copy(k).wait()
+
         values = vbuf[:, pl.ds(pl.multiple_of(k * LANES, LANES), LANES)]
         keys = knorm[k]
-        first = lax.broadcasted_iota(jnp.int32, (tile, LANES), 1) < HDIM
-
-        def attend_tile(i, _):
-            here = pl.ds(pl.multiple_of(i * tile, tile), tile)
-            queries = qbuf[k, here]
-            results = []
-            for mine in (first, jnp.logical_not(first)):
-                masked = jnp.where(mine, queries, jnp.zeros_like(queries))
-                scores = lax.dot_general(
-                    masked, keys, (((1,), (1,)), ((), ())), preferred_element_type=jnp.float32)
-                largest = jnp.max(scores, axis=-1, keepdims=True)
-                probability = jnp.exp2((scores - largest) * exponent)
-                normaliser = jnp.sum(probability, axis=-1, keepdims=True)
-                blended = jnp.dot(
-                    probability.astype(jnp.bfloat16), values, preferred_element_type=jnp.float32)
-                results.append(blended / normaliser)
-            obuf[k, here] = jnp.where(first, results[0], results[1]).astype(jnp.bfloat16)
-            return 0
-
-        lax.fori_loop(0, n * tokens // tile, attend_tile, 0)
-        own_out(k).start()
-        for copy in out_copies(k):
-            copy.start()
+        queries = qbuf[k, here]
+        results = []
+        for mine in (first, jnp.logical_not(first)):
+            masked = jnp.where(mine, queries, jnp.zeros_like(queries))
+            scores = lax.dot_general(
+                masked, keys, (((1,), (1,)), ((), ())), preferred_element_type=jnp.float32)
+            largest = jnp.max(scores, axis=-1, keepdims=True)
+            probability = jnp.exp2((scores - largest) * exponent)
+            normaliser = jnp.sum(probability, axis=-1, keepdims=True)
+            blended = jnp.dot(
+                probability.astype(jnp.bfloat16), values, preferred_element_type=jnp.float32)
+            results.append(blended / normaliser)
+        obuf[k, here] = jnp.where(first, results[0], results[1]).astype(jnp.bfloat16)
+        for core in range(CORES):
+            to = chip * CORES + core
+
+            @pl.when(to != s)
+            def _():
+                out_copy(k, to).start()
+
+            @pl.when(to == s)
+            def _():
+                own_out(k).start()
+
         return 0
 
-    lax.fori_loop(0, chunks, attend_chunk, 0)
+    ready = 2 * early - chunks
+    lax.fori_loop(0, ready * tiles, attend_step, 0)
+    for pair in range(early, chunks):
+        project(pair)
+    lax.fori_loop(ready * tiles, chunks * tiles, attend_step, 0)
 
     def finish(k, _):
         own_out(k).wait()
-        for copy in out_copies(k):
-            copy.wait()
+        for d in range(1, n):
+            out_copy(k, lax.rem(s + d, n)).wait()
         return 0
 
     lax.fori_loop(0, chunks, finish, 0)
@@ -318,7 +381,7 @@
         scratch_shapes=[
             pltpu.VMEM((group, features), bf16),
             pltpu.VMEM((2 * chunks, rows, LANES), jnp.int32),
-            pltpu.VMEM((2 * chunks, features, LANES), bf16),
+            pltpu.VMEM((chunks, features, 2 * LANES), bf16),
             pltpu.VMEM((n * tokens, width), bf16),
             pltpu.VMEM((n * tokens, width), bf16),
             pltpu.VMEM((chunks, n * tokens, LANES), bf16),
@@ -327,7 +390,7 @@
             pltpu.VMEM((chunks, n * tokens, LANES), bf16),
             dma((3,)), dma((2 * chunks,)),
             dma((n,)), dma((n,)), dma((n,)), dma((n,)),
-            dma((2 * chunks, fn)), dma((2 * chunks, fn)),
+            dma((chunks, fn)), dma((chunks, fn)),
             dma((2, n)), dma((2, n)),
             dma((chunks,)), dma((chunks,)),
             dma((chunks, n)), dma((chunks, n)), dma((chunks,)),

time: 88.5 us -> 82.5 us (0.932)
  Pallas kernels: 86.2 us -> 80.1 us
    pallas_call x1, Pallas kernels: 86.2 us -> 80.1 us  [fused_per_device(): pl.pallas_call(functools.partial(fused_kernel, n, fn), out_shape=jax.Shap...]
where the time goes in v2:
time: 82.5 us; the launch traced here: 82.2 us
  Pallas kernels  80.1 us (97%)
  local copies, waits for them, and re-layouts  2.06 us (2%)
    pallas_call x1, Pallas kernels, fused_per_device(): pl.pallas_call(functools.partial(fused_kernel, n, fn), out_shape=jax.Shap...  80.1 us
    unnamed x1, local copies, waits for them, and re-layouts  2.06 us

profile of v2, /device:TPU:0, one launch (start us, length us, event | category | flops | bytes accessed | tf_op | source)
XLA Modules:
  0.0 82.2 jit_solution(4313841065507287591)
XLA Ops:
  0.0 80.1 %shard_map.73 = bf16[128,3072]{1,0:T(8,128)(2,1)} custom-call(bf16[128,3072]{1,0:T(8,128)(2,1)} %bitcast.7, s32[768,3072]{1,0:T(8,128)} %codes.1, f32[6,24]{1,0:T(8,128)} %scales.1, bf16[128,3072]{1,0:T(8,128)(2,1)} %bitcast.8, bf16[128,3072]{1,0:T(8,128)(2,1)} %bitcast.9, f32[1,3072]{1,0:T(1,128)} %bitcast.10, f32[1,3072]{1,0:T(1,128)} %bitcast.11), custom_call_target="tpu_custom_call" | custom-call | tf_op jit(solution)/shard_map/pallas_call | solution.py:376
  80.1 2.1 %copy.9 = bf16[1,128,3072]{2,1,0:T(8,128)(2,1)} copy(bf16[1,128,3072]{2,1,0:T(8,128)(2,1)} %bitcast.6) | data formatting | bytes 1572864

commit v3 on v2

--- a/solution.py
+++ b/solution.py
@@ -94,6 +94,7 @@
 MESH = pl.DeviceIdType.MESH
 LANES = 128
 CORES = 2
+GRID = 2
 
 
 def column_norm(values, gain_row):
@@ -188,7 +189,8 @@
             for step in range(1, n):
                 d = jnp.where(half == 0, step, n - step)
                 to = lax.rem(s + d, n)
-                over_pair = jnp.where(to // m == half, to // CORES != s // CORES, far)
+                to_far = lax.rem(to, m) // CORES == jnp.where(to // m == 0, 0, chips - 1)
+                over_pair = jnp.where(to // m == half, to // CORES != s // CORES, far & to_far)
 
                 @pl.when(over_pair == behind_patches)
                 def _():
@@ -196,14 +198,37 @@
 
     start_kv(False)
 
-    own_rows = pl.ds(pl.multiple_of(f * rows, rows), rows)
-
-    def weight_copies(q):
+    row_mate = f + 1 - 2 * lax.rem(f, GRID)
+    column_mate = lax.rem(f + GRID, fn)
+
+    def weight_copy(pair, way, start, size, to):
+        at = pl.ds(pl.multiple_of(start, size), size)
+        return remote(wbuf.at[pair, at], wbuf.at[pair, at], w_send.at[pair, way], w_recv.at[pair, way], fsdp=to)
+
+    def near_copies(pair):
         return [
-            remote(wbuf.at[q, own_rows], wbuf.at[q, own_rows], w_send.at[q, d], w_recv.at[q, d],
-                   fsdp=lax.rem(f + d, fn))
-            for d in range(1, fn)
+            weight_copy(pair, 0, f * rows, rows, row_mate),
+            weight_copy(pair, 1, f * rows, rows, column_mate),
         ]
+
+    def relay_copies(pair):
+        part = rows // 2
+        return [
+            weight_copy(pair, 2, row_mate * rows, part, column_mate),
+            weight_copy(pair, 3, column_mate * rows + part, part, row_mate),
+        ]
+
+    def relay(pair):
+        for copy in near_copies(pair):
+            copy.wait_recv()
+        for copy in relay_copies(pair):
+            copy.start()
+
+    def relay_early():
+        for pair in range(chunks - 1):
+            relay(pair)
+        for copy in near_copies(chunks - 1):
+            copy.start()
 
     def dequantize_pair(pair, _):
         for side in range(2):
@@ -215,8 +240,12 @@
                 piece = cbuf[q, block * BLOCK:(block + 1) * BLOCK, :].astype(jnp.float32) * scale
                 at = pl.ds(pl.multiple_of(f * rows + block * BLOCK, BLOCK), BLOCK)
                 wbuf[pair, at, side * LANES:(side + 1) * LANES] = piece.astype(jnp.bfloat16)
-        for copy in weight_copies(pair):
-            copy.start()
+
+        @pl.when(pair < chunks - 1)
+        def _():
+            for copy in near_copies(pair):
+                copy.start()
+
         return 0
 
     lax.fori_loop(0, chunks, dequantize_pair, 0)
@@ -240,11 +269,13 @@
     @pl.when(far)
     def _():
         patches_out()
+        relay_early()
         patches_in()
 
     @pl.when(jnp.logical_not(far))
     def _():
         patches_in()
+        relay_early()
 
     patch_copies[0].wait()
     for d in range(1, chips):
@@ -257,7 +288,9 @@
         return remote(qsend.at[k], qbuf.at[k, half_rows], q_send.at[k], q_recv.at[k], seq=other)
 
     def project(pair):
-        for copy in weight_copies(pair):
+        for copy in near_copies(pair):
+            copy.wait_send()
+        for copy in relay_copies(pair):
             copy.wait()
         both = jnp.dot(pbuf[...], wbuf[pair], preferred_element_type=jnp.float32)
         for side in range(2):
@@ -275,6 +308,7 @@
         project(pair)
         if pair == 0:
             pl.when(jnp.logical_not(far))(patches_out)
+    relay(chunks - 1)
 
     own_copies[1].wait()
     for d in range(1, n):
@@ -375,9 +409,9 @@
     vmem = pl.BlockSpec(memory_space=pltpu.VMEM)
     result = pl.pallas_call(
         functools.partial(fused_kernel, n, fn),
-        out_shape=jax.ShapeDtypeStruct((tokens, columns), bf16),
+        out_shape=pltpu.VMEM((tokens, columns), bf16),
         in_specs=[anywhere, anywhere, pl.BlockSpec(memory_space=pltpu.SMEM), anywhere, anywhere, vmem, vmem],
-        out_specs=anywhere,
+        out_specs=vmem,
         scratch_shapes=[
             pltpu.VMEM((group, features), bf16),
             pltpu.VMEM((2 * chunks, rows, LANES), jnp.int32),
@@ -414,7 +448,7 @@
 
     def whole(*arrays):
         patches, weight_codes = arrays[:2]
-        fits = patches.shape[0] == fn and weight_codes.shape[1] % (n * LANES) == 0 and n % (2 * CORES) == 0
+        fits = patches.shape[0] == fn == GRID * GRID and weight_codes.shape[1] % (n * LANES) == 0 and n % (2 * CORES) == 0
         body = functools.partial(fused_per_device, n, fn) if fits else per_device
         return jax.shard_map(
             body, mesh=mesh, in_specs=specs, out_specs=P("fsdp", "seq", None), check_vma=False

time: 82.5 us -> 77.8 us (0.943)
  Pallas kernels: 80.1 us -> 76.7 us
  local copies, waits for them, and re-layouts: 2.06 us -> 0.88 us
    pallas_call x1, Pallas kernels: 80.1 us -> 76.7 us  [fused_per_device(): pl.pallas_call(functools.partial(fused_kernel, n, fn), out_shape=pltpu.VM...]
    unnamed x1, local copies, waits for them, and re-layouts: 2.06 us -> 0.88 us
where the time goes in v3:
time: 77.8 us; the launch traced here: 77.6 us
  Pallas kernels  76.7 us (99%)
  local copies, waits for them, and re-layouts  0.88 us (1%)
    pallas_call x1, Pallas kernels, fused_per_device(): pl.pallas_call(functools.partial(fused_kernel, n, fn), out_shape=pltpu.VM...  76.7 us

profile of v3, /device:TPU:0, one launch (start us, length us, event | category | flops | bytes accessed | tf_op | source)
XLA Modules:
  0.0 77.6 jit_solution(307608278517055553)
XLA Ops:
  0.0 76.7 %shard_map.73 = bf16[128,3072]{1,0:T(8,128)(2,1)S(1)} custom-call(bf16[128,3072]{1,0:T(8,128)(2,1)} %bitcast.7, s32[768,3072]{1,0:T(8,128)} %codes.1, f32[6,24]{1,0:T(8,128)} %scales.1, bf16[128,3072]{1,0:T(8,128)(2,1)} %bitcast.8, bf16[128,3072]{1,0:T(8,128)(2,1)} %bitcast.9, f32[1,3072]{1,0:T(1,128)} %bitcast.10, f32[1,3072]{1,0:T(1,128)} %bitcast.11), custom_call_target="tpu_custom_call" | custom-call | tf_op jit(solution)/shard_map/pallas_call | solution.py:410
  76.7 0.9 %copy.9 = bf16[1,128,3072]{2,1,0:T(8,128)(2,1)} copy(bf16[1,128,3072]{2,1,0:T(8,128)(2,1)S(1)} %bitcast.6) | data formatting | bytes 1572864
